TPU v7x, 32 devices: a whole 2x2x4 slice. The times are simulated.
32 devices in a mesh: seq: 16 (over z, y, x), head: 2 (over core).
Axes of the slice: x: 2, y: 2, z: 4, core: 2. Of those that a mesh axis runs over, the one named last changes fastest.
Arguments:
- query_vectors: bfloat16 [4096, 2560], P(('seq', 'head')), may hold values from -6 to 6
- address_vectors: bfloat16 [4096, 2560], P(('seq', 'head')), may hold values from -0.75 to 0.75
- payload_vectors: bfloat16 [4096, 2560], P(('seq', 'head')), may hold values from -6 to 6
- forget_logarithms: bfloat16 [4096, 2560], P(('seq', 'head')), may hold values from -1.5 to 0
- pre_sigmoid_filter: bfloat16 [4096, 2560], P(('seq', 'head')), may hold values from -6 to 6
- current_reward_table: float32 [40, 64], replicated, may hold values from -0.5 to 1.5
- cluster_standardize_weight: float32 [2560], replicated, may hold values from 0.25 to 1.75
- cluster_standardize_offset: float32 [2560], replicated, may hold values from -1.5 to 1.5
Outputs:
- mixed: bfloat16 [4096, 2560], P('seq', 'head')
All inputs are finite; a program needn't handle non-finite values.
Results may differ from a plain program's by a relative error of at most 0.001.
Values may be sent and summed in bfloat16 or wider, within the bound.
No kernel may reach another device: no remote copies, remote signals or barrier semaphores. Data moves between devices by JAX's collectives and lax.ppermute only.
A program may use at most 192 MiB of HBM per device.

v0:
```python
import math
import jax
import jax.numpy as jnp
from jax import lax
from jax.sharding import PartitionSpec as P

CHANNEL_COUNT = 64


def prefix_2(value, axis, join, neutral):
    count, mine = (lax.axis_size(axis), lax.axis_index(axis))
    pieces = jax.tree.map(lambda part: lax.all_gather(part, axis), value)
    so_far = jax.tree.map(
        lambda part, zero: jnp.full_like(part, 0) + jnp.asarray(zero, part.dtype), value, neutral
    )

    def step(position, so_far):
        longer = join(so_far, jax.tree.map(lambda part: part[position], pieces))
        return jax.tree.map(lambda new, old: jnp.where(position < mine, new, old), longer, so_far)

    return lax.fori_loop(0, count - 1, step, so_far)


def group_heads(array, groups):
    length, hosted_attenders, channels = array.shape
    return array.reshape(length, groups, hosted_attenders // groups, channels).transpose(1, 0, 2, 3)


def block_shares(
    query_vectors, address_vectors, payload_vectors, forget_logarithms, current_reward_piece
):
    length, width = query_vectors.shape
    hosted_attenders = width // CHANNEL_COUNT
    highest = lax.Precision.HIGHEST
    rows = lax.broadcasted_iota(jnp.int32, (length, length), 0)
    columns = lax.broadcasted_iota(jnp.int32, (length, length), 1)
    lower = (rows >= columns).astype(jnp.float32)
    strict = rows > columns
    forget_multiplier = forget_logarithms.astype(jnp.float32)
    cumul = jnp.dot(lower, forget_multiplier, precision=highest)
    before = (cumul - forget_multiplier).reshape(length, hosted_attenders, CHANNEL_COUNT)
    final = cumul[-1].reshape(hosted_attenders, CHANNEL_COUNT)
    cumul = cumul.reshape(length, hosted_attenders, CHANNEL_COUNT)
    incoming_memory = query_vectors.astype(jnp.float32).reshape(
        length, hosted_attenders, CHANNEL_COUNT
    )
    address_block = address_vectors.astype(jnp.float32).reshape(
        length, hosted_attenders, CHANNEL_COUNT
    )
    payload_block = payload_vectors.astype(jnp.float32).reshape(
        length, hosted_attenders, CHANNEL_COUNT
    )
    scaled_receptance = incoming_memory * jnp.exp(before)
    scaled_k = address_block * jnp.exp(-cumul)
    end_keys = address_block * jnp.exp(final[None] - cumul)
    group_size = math.gcd(hosted_attenders, 4)
    groups = hosted_attenders // group_size

    def group_output(pieces):
        receptance_group, keys_group, values_group = pieces
        scores = jnp.einsum("thc,shc->hts", receptance_group, keys_group, precision=highest)
        scores = jnp.where(strict[None], scores, jnp.float32(0.0))
        return jnp.einsum("hts,shj->thj", scores, values_group, precision=highest)

    grouped = lax.map(
        group_output,
        (
            group_heads(scaled_receptance, groups),
            group_heads(scaled_k, groups),
            group_heads(payload_block, groups),
        ),
    )
    within = grouped.transpose(1, 0, 2, 3).reshape(length, hosted_attenders, CHANNEL_COUNT)
    diagonal_piece = jnp.sum(incoming_memory * current_reward_piece[None] * address_block, axis=2)
    mixed_output = within + diagonal_piece[:, :, None] * payload_block
    slab_ends = jnp.einsum("shc,shj->hcj", end_keys, payload_block, precision=highest)
    return (mixed_output, scaled_receptance, jnp.exp(final), slab_ends)


def join_states(earlier, later):
    return (earlier[0] * later[0], later[0][:, :, None] * earlier[1] + later[1])


def finish(mixed_output, scaled_receptance, prefix, pre_sigmoid_filter, gain, bias):
    mixed_output = mixed_output + jnp.einsum(
        "thc,hcj->thj", scaled_receptance, prefix, precision=lax.Precision.HIGHEST
    )
    length = mixed_output.shape[0]
    center = mixed_output - jnp.mean(mixed_output, axis=2, keepdims=True)
    spread = jnp.mean(center * center, axis=2, keepdims=True)
    normed = (center * lax.rsqrt(spread + 1e-05)).reshape(length, -1)
    gate = pre_sigmoid_filter.astype(jnp.float32)
    return ((normed * gain[None] + bias[None]) * gate * jax.nn.sigmoid(gate)).astype(jnp.bfloat16)


def body(
    query_vectors,
    address_vectors,
    payload_vectors,
    forget_logarithms,
    pre_sigmoid_filter,
    current_reward_table,
    cluster_standardize_weight,
    cluster_standardize_offset,
):
    incoming_memory, address_block, payload_block, forget_multiplier, gate = (
        lax.all_to_all(query_vectors, "head", split_axis=1, concat_axis=0, tiled=True),
        lax.all_to_all(address_vectors, "head", split_axis=1, concat_axis=0, tiled=True),
        lax.all_to_all(payload_vectors, "head", split_axis=1, concat_axis=0, tiled=True),
        lax.all_to_all(forget_logarithms, "head", split_axis=1, concat_axis=0, tiled=True),
        lax.all_to_all(pre_sigmoid_filter, "head", split_axis=1, concat_axis=0, tiled=True),
    )
    width = incoming_memory.shape[1]
    hosted_attenders = width // CHANNEL_COUNT
    block_offset = lax.axis_index("head")
    current_reward_piece = lax.dynamic_slice_in_dim(
        current_reward_table, block_offset * hosted_attenders, hosted_attenders, 0
    )
    gain = lax.dynamic_slice_in_dim(cluster_standardize_weight, block_offset * width, width, 0)
    bias = lax.dynamic_slice_in_dim(cluster_standardize_offset, block_offset * width, width, 0)
    mixed_output, scaled_receptance, decay_total, slab_ends = block_shares(
        incoming_memory, address_block, payload_block, forget_multiplier, current_reward_piece
    )
    identity = (jnp.ones_like(decay_total), jnp.zeros_like(slab_ends))
    carried = prefix_2((decay_total, slab_ends), "seq", join_states, identity)
    return finish(mixed_output, scaled_receptance, carried[1], gate, gain, bias)


def solution(mesh):
    return jax.shard_map(
        body,
        mesh=mesh,
        in_specs=(
            P(("seq", "head"), None),
            P(("seq", "head"), None),
            P(("seq", "head"), None),
            P(("seq", "head"), None),
            P(("seq", "head"), None),
            P(),
            P(),
            P(),
        ),
        out_specs=P("seq", "head"),
        check_vma=False,
    )
```

profile of v0, /device:TPU:0, one launch (start us, length us, event | category | flops | bytes accessed | tf_op | source)
XLA Modules:
  0.0 217.2 jit_solution(4822067310482961612)
XLA Ops:
  8.6 3.5 %all-to-all-start.2 = ((bf16[128,2,1280]{2,0,1:T(8,128)(2,1)}), bf16[128,2,1280]{2,0,1:T(8,128)(2,1)S(1)}, u32[]{:S(2)}, u32[]{:S(2)}) async-start(bf16[128,2,1280]{2,0,1:T(8,128)(2,1)} %bitcast.92), calls=%async_computation.2 | async-start | bytes 1310720 | tf_op jit(solution)/shard_map/all_to_all | solution.py:110
  13.9 3.5 %all-to-all-start.3 = ((bf16[128,2,1280]{0,2,1:T(8,128)(2,1)}), bf16[128,2,1280]{0,2,1:T(8,128)(2,1)S(1)}, u32[]{:S(2)}, u32[]{:S(2)}) async-start(bf16[128,2,1280]{0,2,1:T(8,128)(2,1)} %bitcast.10), calls=%async_computation.3 | async-start | bytes 1310720 | tf_op jit(solution)/shard_map/all_to_all | solution.py:108
  22.0 3.5 %all-to-all-start = ((bf16[128,2,1280]{0,2,1:T(8,128)(2,1)}), bf16[128,2,1280]{0,2,1:T(8,128)(2,1)S(1)}, u32[]{:S(2)}, u32[]{:S(2)}) async-start(bf16[128,2,1280]{0,2,1:T(8,128)(2,1)} %bitcast), calls=%async_computation | async-start | bytes 1310720 | tf_op jit(solution)/shard_map/all_to_all | solution.py:109
  25.7 4.8 %copy.56 = f32[2,128,1280]{1,0,2:T(2,128)S(1)} copy(f32[2,128,1280]{1,2,0:T(8,128)S(1)} %convert_bitcast_fusion) | data formatting | bytes 2621440 | tf_op jit(solution)/shard_map/convert_element_type | solution.py:47
  32.4 6.1 %copy.60 = bf16[2,128,1280]{1,0,2:T(2,128)(2,1)} copy(bf16[2,128,1280]{1,2,0:T(8,128)(2,1)S(1)} %bitcast.110) | data formatting | bytes 1310720 | tf_op jit(solution)/shard_map/all_to_all | solution.py:109
  38.5 2.2 %all_to_all.69 = bf16[256,20,64]{0,2,1:T(8,128)(2,1)S(1)} reshape(bf16[2,128,1280]{1,0,2:T(2,128)(2,1)} %copy.60) | data formatting | bytes 1310720 | tf_op jit(solution)/shard_map/all_to_all | solution.py:109
  40.8 3.3 %fusion.22 = f32[20,64,64]{2,1,0:T(8,128)} fusion(bf16[256,20,64]{0,2,1:T(8,128)(2,1)S(1)} %all_to_all.69, f32[256,20,64]{0,2,1:T(8,128)S(1)} %reshape.91, f32[256,20,64]{0,2,1:T(8,128)} %bitcast.111, f32[20,64]{1,0:T(8,128)S(1)} %sub.22), kind=kOutput, calls=%fused_computation.32 | convolution fusion | flops 252313600 | bytes 3609600 | tf_op jit(solution)/shard_map/shc,shj->hcj/dot_general | solution.py:76
  44.1 2.2 %copy.51 = bf16[128,2560]{0,1:T(8,128)(2,1)} copy(bf16[128,2560]{1,0:T(8,128)(2,1)} %param.12) | data formatting | bytes 1310720 | tf_op args[0]
  46.3 3.7 %all-to-all-start.1 = ((bf16[128,2,1280]{0,2,1:T(8,128)(2,1)}), bf16[128,2,1280]{0,2,1:T(8,128)(2,1)S(1)}, u32[]{:S(2)}, u32[]{:S(2)}) async-start(bf16[128,2,1280]{0,2,1:T(8,128)(2,1)} %bitcast.3), calls=%async_computation.1 | async-start | bytes 1310720 | tf_op jit(solution)/shard_map/all_to_all | solution.py:107
  50.0 2.1 reshape.89
  54.1 4.3 %all-to-all-start.4 = ((bf16[128,2,1280]{2,0,1:T(8,128)(2,1)}), bf16[128,2,1280]{2,0,1:T(8,128)(2,1)}, u32[]{:S(2)}, u32[]{:S(2)}) async-start(bf16[128,2,1280]{2,0,1:T(8,128)(2,1)} %bitcast.91), calls=%async_computation.4 | async-start | bytes 1310720 | tf_op jit(solution)/shard_map/all_to_all | solution.py:111
  58.5 4.8 %copy.52 = f32[2,128,1280]{1,0,2:T(2,128)S(1)} copy(f32[2,128,1280]{1,2,0:T(8,128)S(1)} %convert_bitcast_fusion.1) | data formatting | bytes 2621440 | tf_op jit(solution)/shard_map/convert_element_type | solution.py:44
  64.3 2.1 reshape.88
  66.5 2.3 %reshape.90 = f32[256,20,64]{0,2,1:T(8,128)S(1)} reshape(f32[2,128,1280]{1,0,2:T(2,128)} %copy-done.1) | data formatting | bytes 2621440 | tf_op jit(solution)/shard_map/convert_element_type | solution.py:44
  68.8 2.8 %copy.54 = f32[256,1280]{0,1:T(8,128)} copy(f32[256,1280]{1,0:T(8,128)} %get-tuple-element.191) | data formatting | bytes 2621440 | tf_op jit(solution)/shard_map/exp | solution.py:53
  71.6 2.8 %copy.57 = f32[256,1280]{0,1:T(8,128)} copy(f32[256,1280]{1,0:T(8,128)} %get-tuple-element.190) | data formatting | bytes 2621440 | tf_op jit(solution)/shard_map/exp | solution.py:54
  75.6 5.6 %copy.50 = f32[2,128,1280]{1,0,2:T(2,128)} copy(f32[2,128,1280]{1,2,0:T(8,128)S(1)} %bitcast_convert_fusion) | data formatting | bytes 2621440 | tf_op jit(solution)/shard_map/transpose | solution.py:26
  81.2 3.1 %reshape.93 = f32[256,5,4,64]{0,3,2,1:T(8,128)} reshape(f32[2,128,1280]{1,0,2:T(2,128)} %copy.50) | data formatting | bytes 2621440 | tf_op jit(solution)/shard_map/transpose | solution.py:26
  84.6 45.8 %all_gather.10 = f32[16,20,64]{2,1,0:T(8,128)S(1)} all-gather(f32[1,20,64]{2,1,0:T(8,128)S(1)} %exp.41), channel_id=1, replica_groups=mesh['seq'=16,'head'=2] {'seq'}, dimensions={0}, use_global_device_ids=true | all-gather | bytes 87040 | tf_op jit(solution)/shard_map/all_gather | solution.py:12
  130.4 3.2 %multiply_bitcast_fusion.1 = f32[5,256,4,64]{1,3,2,0:T(8,128)} fusion(f32[256,5,4,64]{0,3,2,1:T(8,128)} %reshape.88, f32[256,5,4,64]{0,3,2,1:T(8,128)} %bitcast.107), kind=kLoop, calls=%fused_computation.39 | loop fusion | flops 327680 | bytes 3932160 | tf_op jit(solution)/shard_map/transpose | solution.py:26
  134.8 24.7 %while.25 = (s32[]{:T(128)}, f32[5,256,4,64]{1,3,2,0:T(8,128)}, f32[5,256,4,64]{1,3,2,0:T(8,128)}, f32[5,256,4,64]{1,3,2,0:T(8,128)}, f32[5,256,4,64]{1,3,2,0:T(8,128)}, /*index=5*/s32[]{:T(128)}) while((s32[]{:T(128)}, f32[5,256,4,64]{1,3,2,0:T(8,128)}, f32[5,256,4,64]{1,3,2,0:T(8,128)}, f32[5,256,4,64]{1,3,2,0:T(8,128)}, ...), condition=%wide.region_1.2_spmd.clone, body=%wide.region_0.1_spmd.clone.sunk | while | flops 402980864 | bytes 3278917 | solution.py:65
  136.9 2.8 %fusion.44 = f32[5,256,4,64]{1,3,2,0:T(8,128)} fusion(f32[5,256,4,64]{1,3,2,0:T(8,128)} %get-tuple-element.264, s32[]{:T(128)} %get-tuple-element.263, f32[4,256,256]{2,1,0:T(8,128)S(1)} %convolution_select_fusion.2, f32[5,256,4,64]{1,3,2,0:T(8,128)} %get-tuple-element.271), kind=kOutput, calls=%fused_computation.3.clone.1 | convolution fusion | flops 201326592 | bytes 1573888 | tf_op jit(solution)/shard_map/while/body/eval_jaxpr/hts,shj->thj/dot_general | solution.py:63
  139.7 2.1 convolution_select_fusion.2
  141.8 2.8 %fusion.44 = f32[5,256,4,64]{1,3,2,0:T(8,128)} fusion(f32[5,256,4,64]{1,3,2,0:T(8,128)} %get-tuple-element.264, s32[]{:T(128)} %get-tuple-element.263, f32[4,256,256]{2,1,0:T(8,128)S(1)} %convolution_select_fusion.2, f32[5,256,4,64]{1,3,2,0:T(8,128)} %get-tuple-element.271), kind=kOutput, calls=%fused_computation.3.clone.1 | convolution fusion | flops 201326592 | bytes 1573888 | tf_op jit(solution)/shard_map/while/body/eval_jaxpr/hts,shj->thj/dot_general | solution.py:63
  146.8 2.8 %fusion.44 = f32[5,256,4,64]{1,3,2,0:T(8,128)} fusion(f32[5,256,4,64]{1,3,2,0:T(8,128)} %get-tuple-element.264, s32[]{:T(128)} %get-tuple-element.263, f32[4,256,256]{2,1,0:T(8,128)S(1)} %convolution_select_fusion.2, f32[5,256,4,64]{1,3,2,0:T(8,128)} %get-tuple-element.271), kind=kOutput, calls=%fused_computation.3.clone.1 | convolution fusion | flops 201326592 | bytes 1573888 | tf_op jit(solution)/shard_map/while/body/eval_jaxpr/hts,shj->thj/dot_general | solution.py:63
  151.7 2.8 %fusion.44 = f32[5,256,4,64]{1,3,2,0:T(8,128)} fusion(f32[5,256,4,64]{1,3,2,0:T(8,128)} %get-tuple-element.264, s32[]{:T(128)} %get-tuple-element.263, f32[4,256,256]{2,1,0:T(8,128)S(1)} %convolution_select_fusion.2, f32[5,256,4,64]{1,3,2,0:T(8,128)} %get-tuple-element.271), kind=kOutput, calls=%fused_computation.3.clone.1 | convolution fusion | flops 201326592 | bytes 1573888 | tf_op jit(solution)/shard_map/while/body/eval_jaxpr/hts,shj->thj/dot_general | solution.py:63
  156.6 2.8 %fusion.44 = f32[5,256,4,64]{1,3,2,0:T(8,128)} fusion(f32[5,256,4,64]{1,3,2,0:T(8,128)} %get-tuple-element.264, s32[]{:T(128)} %get-tuple-element.263, f32[4,256,256]{2,1,0:T(8,128)S(1)} %convolution_select_fusion.2, f32[5,256,4,64]{1,3,2,0:T(8,128)} %get-tuple-element.271), kind=kOutput, calls=%fused_computation.3.clone.1 | convolution fusion | flops 201326592 | bytes 1573888 | tf_op jit(solution)/shard_map/while/body/eval_jaxpr/hts,shj->thj/dot_general | solution.py:63
  159.4 3.1 %fusion.15 = f32[256,20,64]{0,2,1:T(8,128)} fusion(f32[256,20,64]{0,2,1:T(8,128)} %bitcast.15, bf16[256,20,64]{0,2,1:T(8,128)(2,1)} %copy-done.3, f32[256,20,64]{0,2,1:T(8,128)S(1)} %reshape.91, f32[256,20,64]{0,2,1:T(8,128)S(1)} %reshape.90, f32[20,64]{1,0:T(8,128)S(1)} %constant_dynamic-slice_fusion), kind=kOutput, calls=%fused_computation.20 | output fusion | flops 1643583 | bytes 5903360 | tf_op jit(solution)/shard_map/mul | solution.py:75
  162.5 18.6 %all-gather.3.cloned.1.call-done = f32[320,64,64]{2,1,0:T(8,128)} async-done(((f32[20,64,64]{2,1,0:T(8,128)}), f32[320,64,64]{2,1,0:T(8,128)}) %all-gather.3.cloned.1.call-update) | async-done | bytes 5242896 | tf_op jit(solution)/shard_map/all_gather | solution.py:12
  181.1 23.3 %while.26 = (s32[]{:T(128)}, f32[20,64,64]{2,1,0:T(8,128)S(1)}, s32[]{:T(128)}, f32[16,20,64]{2,1,0:T(8,128)S(1)}, f32[16,20,64,64]{3,2,1,0:T(8,128)}, /*index=5*/s32[]{:T(128)}, s32[]{:T(128)}) while((s32[]{:T(128)}, f32[20,64,64]{2,1,0:T(8,128)S(1)}, s32[]{:T(128)}, f32[16,20,64]{2,1,0:T(8,128)S(1)}, ...), condition=%wide.region_4.5_spmd.clone, body=%wide.region_3.4_spmd.clone.sunk | while | flops 327684 | bytes 998505 | solution.py:21
  204.5 2.7 %fusion.29 = (f32[256,20]{0,1:T(8,128)S(1)}, f32[256,20,64]{0,2,1:T(8,128)S(1)}) fusion(f32[256,20,64]{0,2,1:T(8,128)} %fusion.15, f32[20,64,64]{2,1,0:T(8,128)S(1)} %get-tuple-element.132, f32[256,20,64]{0,2,1:T(8,128)S(1)} %reshape.90, f32[256,20,64]{0,2,1:T(8,128)S(1)} %bitcast.108), kind=kOutput, calls=%fused_computation.54 | convolution fusion | flops 252636160 | bytes 5591040 | tf_op jit(solution)/shard_map/thc,hcj->thj/dot_general | solution.py:85
  208.0 2.4 %fusion.17 = bf16[256,1280]{1,0:T(8,128)(2,1)} fusion(bf16[128,2,1280]{2,0,1:T(8,128)(2,1)} %all-to-all-done.4, f32[256,1280]{1,0:T(8,128)S(1)} %copy.64, f32[1280]{0:T(1024)S(1)} %dynamic_slice.35, f32[1280]{0:T(1024)S(1)} %dynamic_slice.34), kind=kLoop, calls=%fused_computation.24 | loop fusion | flops 2949120 | bytes 2631680 | tf_op jit(solution)/shard_map/convert_element_type | solution.py:93
  (92 shorter events, 48.4 us)
Async XLA Ops:
  6.5 123.8 %copy-start = (f32[40,64]{1,0:T(8,128)S(1)}, f32[40,64]{1,0:T(8,128)}, u32[]{:S(2)}) copy-start(f32[40,64]{1,0:T(8,128)} %param.17) | copy-start | bytes 30724
  6.5 5.6 %copy-start.7 = (bf16[128,2560]{1,0:T(8,128)(2,1)S(1)}, bf16[128,2560]{1,0:T(8,128)(2,1)}, u32[]{:S(2)}) copy-start(bf16[128,2560]{1,0:T(8,128)(2,1)} %param.13) | copy-start | bytes 1966084
  8.6 5.3 %all-to-all-start.2 = ((bf16[128,2,1280]{2,0,1:T(8,128)(2,1)}), bf16[128,2,1280]{2,0,1:T(8,128)(2,1)S(1)}, u32[]{:S(2)}, u32[]{:S(2)}) async-start(bf16[128,2,1280]{2,0,1:T(8,128)(2,1)} %bitcast.92), calls=%async_computation.2 | async-start | bytes 1310720 | tf_op jit(solution)/shard_map/all_to_all | solution.py:110
  13.9 8.1 %all-to-all-start.3 = ((bf16[128,2,1280]{0,2,1:T(8,128)(2,1)}), bf16[128,2,1280]{0,2,1:T(8,128)(2,1)S(1)}, u32[]{:S(2)}, u32[]{:S(2)}) async-start(bf16[128,2,1280]{0,2,1:T(8,128)(2,1)} %bitcast.10), calls=%async_computation.3 | async-start | bytes 1310720 | tf_op jit(solution)/shard_map/all_to_all | solution.py:108
  19.5 1.5 copy-start.8
  22.0 9.5 %all-to-all-start = ((bf16[128,2,1280]{0,2,1:T(8,128)(2,1)}), bf16[128,2,1280]{0,2,1:T(8,128)(2,1)S(1)}, u32[]{:S(2)}, u32[]{:S(2)}) async-start(bf16[128,2,1280]{0,2,1:T(8,128)(2,1)} %bitcast), calls=%async_computation | async-start | bytes 1310720 | tf_op jit(solution)/shard_map/all_to_all | solution.py:109
  25.6 155.6 %all-gather.3.cloned.1.call-start = ((), (), s32[]{:S(2)}) async-start(), calls=%async_computation.5 | async-start | bytes 11141120 | tf_op jit(solution)/shard_map/all_gather | solution.py:12
  31.5 0.8 copy-start.4
  40.7 3.4 %copy-start.3 = (bf16[256,20,64]{0,2,1:T(8,128)(2,1)}, bf16[256,20,64]{0,2,1:T(8,128)(2,1)S(1)}, u32[]{:S(2)}) copy-start(bf16[256,20,64]{0,2,1:T(8,128)(2,1)S(1)} %all_to_all.69) | copy-start | bytes 1966084
  46.3 7.8 %all-to-all-start.1 = ((bf16[128,2,1280]{0,2,1:T(8,128)(2,1)}), bf16[128,2,1280]{0,2,1:T(8,128)(2,1)S(1)}, u32[]{:S(2)}, u32[]{:S(2)}) async-start(bf16[128,2,1280]{0,2,1:T(8,128)(2,1)} %bitcast.3), calls=%async_computation.1 | async-start | bytes 1310720 | tf_op jit(solution)/shard_map/all_to_all | solution.py:107
  54.1 153.9 %all-to-all-start.4 = ((bf16[128,2,1280]{2,0,1:T(8,128)(2,1)}), bf16[128,2,1280]{2,0,1:T(8,128)(2,1)}, u32[]{:S(2)}, u32[]{:S(2)}) async-start(bf16[128,2,1280]{2,0,1:T(8,128)(2,1)} %bitcast.91), calls=%async_computation.4 | async-start | bytes 1310720 | tf_op jit(solution)/shard_map/all_to_all | solution.py:111
  63.2 1.1 copy-start.1
  81.2 3.2 %copy-start.9 = (f32[2560]{0:T(1024)S(1)}, f32[2560]{0:T(1024)}, u32[]{:S(2)}) copy-start(f32[2560]{0:T(1024)} %param.18) | copy-start | bytes 30724
  81.2 3.3 %copy-start.10 = (f32[2560]{0:T(1024)S(1)}, f32[2560]{0:T(1024)}, u32[]{:S(2)}) copy-start(f32[2560]{0:T(1024)} %param.19) | copy-start | bytes 30724
  130.4 3.2 %copy-start.5 = (f32[256,5,4,64]{0,3,2,1:T(8,128)S(1)}, f32[256,5,4,64]{0,3,2,1:T(8,128)}, u32[]{:S(2)}) copy-start(f32[256,5,4,64]{0,3,2,1:T(8,128)} %reshape.89) | copy-start | bytes 3932164
  130.4 3.2 %copy-start.6 = (f32[256,1280]{0,1:T(8,128)S(1)}, f32[256,1280]{0,1:T(8,128)}, u32[]{:S(2)}) copy-start(f32[256,1280]{0,1:T(8,128)} %copy.57) | copy-start | bytes 3932164
  181.1 23.3 %copy-start.2 = (f32[256,1280]{0,1:T(8,128)S(1)}, f32[256,1280]{0,1:T(8,128)}, u32[]{:S(2)}) copy-start(f32[256,1280]{0,1:T(8,128)} %copy.54) | copy-start | bytes 3932164
Sparse Core Ops, SparseCore 0:
  44.2 136.8 all-gather.2
where the time goes:
time: 219 us; the launch traced here: 217 us
  local copies, waits for them, and re-layouts  52.5 us (24%)
  blocking collectives  45.8 us (21%)
  other arithmetic  34.4 us (16%)
  matrix products  32.5 us (15%)
  waiting for transfers between devices  19.3 us (9%)
  starting transfers between devices  18.5 us (8%)
  between operations  13.7 us (6%)
    all_gather x1, blocking collectives, prefix_2(): pieces = jax.tree.map(lambda part: lax.all_gather(part, axis), value)  45.8 us
    select_n x15, other arithmetic, step(): jnp.where(position < mine, new, old)  22.7 us
    all_gather x1, waiting for transfers between devices, prefix_2(): pieces = jax.tree.map(lambda part: lax.all_gather(part, axis), value)  18.6 us
    dot_general x5, matrix products, group_output(): return jnp.einsum('hts,shj->thj', scores, values_group, precision=highest)  13.9 us
    dot_general x5, matrix products, group_output(): jnp.einsum('thc,shc->hts', receptance_group, keys_group, precision=highest)  10.6 us
    convert_element_type x3, local copies, waits for them, and re-layouts, block_shares(): query_vectors.astype(jnp.float32)  9.25 us
    transpose x2, local copies, waits for them, and re-layouts, group_heads(): array.reshape(length, groups, hosted_attenders // groups, channels)  8.76 us
    all_to_all x2, local copies, waits for them, and re-layouts, body(): lax.all_to_all(payload_vectors, 'head', split_axis=1, concat_axis=0, tile...  8.34 us
  transfers between devices with their start and end apart: 6, of which 2 were waited for; matrix products, arithmetic and copies ran while one was open for 47% of the time, Pallas kernels for 0%

commit v1 on v0

--- a/solution.py
+++ b/solution.py
@@ -106,7 +106,12 @@
     incoming_memory, address_block, payload_block, forget_multiplier, gate = (
         lax.all_to_all(query_vectors, "head", split_axis=1, concat_axis=0, tiled=True),
         lax.all_to_all(address_vectors, "head", split_axis=1, concat_axis=0, tiled=True),
-        lax.all_to_all(payload_vectors, "head", split_axis=1, concat_axis=0, tiled=True),
+        jnp.concatenate(
+            lax.all_to_all(
+                jnp.stack(jnp.split(payload_vectors, lax.axis_size("head"), axis=1)), "head", 0, 0
+            ),
+            axis=0,
+        ),
         lax.all_to_all(forget_logarithms, "head", split_axis=1, concat_axis=0, tiled=True),
         lax.all_to_all(pre_sigmoid_filter, "head", split_axis=1, concat_axis=0, tiled=True),
     )

time: 219 us -> 212 us (0.968)
  local copies, waits for them, and re-layouts: 52.5 us -> 41 us
  waiting for transfers between devices: 19.3 us -> 24.2 us
    all_to_all x2 -> x1, local copies, waits for them, and re-layouts: 8.34 us -> 0.93 us  [body(): lax.all_to_all(jnp.stack(jnp.split(payload_vectors, lax.axis_size('head')...]
    all_gather x1, waiting for transfers between devices: 18.6 us -> 23.4 us  [prefix_2(): pieces = jax.tree.map(lambda part: lax.all_gather(part, axis), value)]
    transpose x2, local copies, waits for them, and re-layouts: 8.76 us -> 6.14 us  [group_heads(): array.reshape(length, groups, hosted_attenders // groups, channels)]
    unnamed x25 -> x22, local copies, waits for them, and re-layouts: 6.28 us -> 4.37 us
    transpose x3 -> x2, other arithmetic: 5.56 us -> 4.4 us  [group_heads(): array.reshape(length, groups, hosted_attenders // groups, channels)]
  transfers between devices with their start and end apart: 6 -> 6, of which waited for: 2 -> 2; matrix products, arithmetic and copies ran while one was open for 47% -> 46% of each run, Pallas kernels for 0% -> 0%
where the time goes in v1:
time: 212 us; the launch traced here: 210 us
  blocking collectives  45.5 us (21%)
  local copies, waits for them, and re-layouts  41 us (19%)
  other arithmetic  33.8 us (16%)
  matrix products  32.8 us (15%)
  waiting for transfers between devices  24.2 us (11%)
  starting transfers between devices  18.6 us (9%)
  between operations  13.7 us (6%)
    all_gather x1, blocking collectives, prefix_2(): pieces = jax.tree.map(lambda part: lax.all_gather(part, axis), value)  45.5 us
    all_gather x1, waiting for transfers between devices, prefix_2(): pieces = jax.tree.map(lambda part: lax.all_gather(part, axis), value)  23.4 us
    select_n x15, other arithmetic, step(): jnp.where(position < mine, new, old)  22.6 us
    dot_general x5, matrix products, group_output(): return jnp.einsum('hts,shj->thj', scores, values_group, precision=highest)  13.9 us
    dot_general x5, matrix products, group_output(): jnp.einsum('thc,shc->hts', receptance_group, keys_group, precision=highest)  10.6 us
    convert_element_type x3, local copies, waits for them, and re-layouts, block_shares(): query_vectors.astype(jnp.float32)  9.24 us
    convert_element_type x3, local copies, waits for them, and re-layouts, block_shares(): address_vectors.astype(jnp.float32)  7.94 us
    transpose x2, local copies, waits for them, and re-layouts, group_heads(): array.reshape(length, groups, hosted_attenders // groups, channels)  6.14 us
  transfers between devices with their start and end apart: 6, of which 2 were waited for; matrix products, arithmetic and copies ran while one was open for 46% of the time, Pallas kernels for 0%

profile of v1, /device:TPU:0, one launch (start us, length us, event | category | flops | bytes accessed | tf_op | source)
XLA Modules:
  0.0 210.1 jit_solution(12797497382640444796)
XLA Ops:
  8.6 3.5 %all-to-all-start.2 = ((bf16[128,2,1280]{2,0,1:T(8,128)(2,1)}), bf16[128,2,1280]{2,0,1:T(8,128)(2,1)S(1)}, u32[]{:S(2)}, u32[]{:S(2)}) async-start(bf16[128,2,1280]{2,0,1:T(8,128)(2,1)} %bitcast.93), calls=%async_computation.2 | async-start | bytes 1310720 | tf_op jit(solution)/shard_map/all_to_all | solution.py:115
  13.9 3.5 %all-to-all-start.3 = ((bf16[128,2,1280]{0,2,1:T(8,128)(2,1)}), bf16[128,2,1280]{0,2,1:T(8,128)(2,1)S(1)}, u32[]{:S(2)}, u32[]{:S(2)}) async-start(bf16[128,2,1280]{0,2,1:T(8,128)(2,1)} %bitcast.10), calls=%async_computation.3 | async-start | bytes 1310720 | tf_op jit(solution)/shard_map/all_to_all | solution.py:108
  21.9 3.5 %all-to-all-start = ((bf16[2,128,1280]{2,1,0:T(8,128)(2,1)}), bf16[2,128,1280]{2,1,0:T(8,128)(2,1)S(1)}, u32[]{:S(2)}, u32[]{:S(2)}) async-start(bf16[2,128,1280]{2,1,0:T(8,128)(2,1)} %pad_maximum_fusion), calls=%async_computation | async-start | bytes 1310720 | tf_op jit(solution)/shard_map/all_to_all | solution.py:110
  25.6 4.8 %copy.41 = f32[2,128,1280]{1,0,2:T(2,128)S(1)} copy(f32[2,128,1280]{1,2,0:T(8,128)S(1)} %convert_bitcast_fusion) | data formatting | bytes 2621440 | tf_op jit(solution)/shard_map/convert_element_type | solution.py:47
  32.9 3.1 %fusion.22 = f32[20,64,64]{2,1,0:T(8,128)} fusion(bf16[256,20,64]{0,2,1:T(8,128)(2,1)S(1)} %reshape.86, f32[256,20,64]{0,2,1:T(8,128)S(1)} %reshape.92, f32[256,20,64]{0,2,1:T(8,128)} %bitcast.111, f32[20,64]{1,0:T(8,128)S(1)} %sub.22), kind=kOutput, calls=%fused_computation.32 | convolution fusion | flops 252313600 | bytes 3609600 | tf_op jit(solution)/shard_map/shc,shj->hcj/dot_general | solution.py:76
  36.0 2.2 %copy.36 = bf16[128,2560]{0,1:T(8,128)(2,1)} copy(bf16[128,2560]{1,0:T(8,128)(2,1)} %param.12) | data formatting | bytes 1310720 | tf_op args[0]
  38.2 3.5 %all-to-all-start.1 = ((bf16[128,2,1280]{0,2,1:T(8,128)(2,1)}), bf16[128,2,1280]{0,2,1:T(8,128)(2,1)S(1)}, u32[]{:S(2)}, u32[]{:S(2)}) async-start(bf16[128,2,1280]{0,2,1:T(8,128)(2,1)} %bitcast.3), calls=%async_computation.1 | async-start | bytes 1310720 | tf_op jit(solution)/shard_map/all_to_all | solution.py:107
  41.7 2.1 %reshape.90 = f32[256,5,4,64]{0,3,2,1:T(8,128)} reshape(f32[2,128,1280]{1,0,2:T(2,128)S(1)} %copy.41) | data formatting | bytes 2621440 | tf_op jit(solution)/shard_map/convert_element_type | solution.py:47
  45.8 4.5 %all-to-all-start.4 = ((bf16[128,2,1280]{2,0,1:T(8,128)(2,1)}), bf16[128,2,1280]{2,0,1:T(8,128)(2,1)}, u32[]{:S(2)}, u32[]{:S(2)}) async-start(bf16[128,2,1280]{2,0,1:T(8,128)(2,1)} %bitcast.92), calls=%async_computation.4 | async-start | bytes 1310720 | tf_op jit(solution)/shard_map/all_to_all | solution.py:116
  50.4 4.8 %copy.37 = f32[2,128,1280]{1,0,2:T(2,128)S(1)} copy(f32[2,128,1280]{1,2,0:T(8,128)S(1)} %convert_bitcast_fusion.1) | data formatting | bytes 2621440 | tf_op jit(solution)/shard_map/convert_element_type | solution.py:44
  56.2 2.1 %reshape.89 = f32[256,5,4,64]{0,3,2,1:T(8,128)} reshape(f32[2,128,1280]{1,0,2:T(2,128)S(1)} %copy.37) | data formatting | bytes 2621440 | tf_op jit(solution)/shard_map/convert_element_type | solution.py:44
  58.4 2.3 %reshape.91 = f32[256,20,64]{0,2,1:T(8,128)S(1)} reshape(f32[2,128,1280]{1,0,2:T(2,128)} %copy-done.1) | data formatting | bytes 2621440 | tf_op jit(solution)/shard_map/convert_element_type | solution.py:44
  60.7 2.8 %copy.39 = f32[256,1280]{0,1:T(8,128)} copy(f32[256,1280]{1,0:T(8,128)} %get-tuple-element.191) | data formatting | bytes 2621440 | tf_op jit(solution)/shard_map/exp | solution.py:53
  63.5 2.8 %copy.42 = f32[256,1280]{0,1:T(8,128)} copy(f32[256,1280]{1,0:T(8,128)} %get-tuple-element.190) | data formatting | bytes 2621440 | tf_op jit(solution)/shard_map/exp | solution.py:54
  66.3 3.0 %copy.35 = f32[2,128,1280]{1,0,2:T(2,128)} copy(bf16[2,128,1280]{2,1,0:T(8,128)(2,1)} %copy-done.3) | data formatting | bytes 1966080 | tf_op jit(solution)/shard_map/transpose | solution.py:26
  69.3 3.1 %reshape.94 = f32[256,5,4,64]{0,3,2,1:T(8,128)} reshape(f32[2,128,1280]{1,0,2:T(2,128)} %copy.35) | data formatting | bytes 2621440 | tf_op jit(solution)/shard_map/transpose | solution.py:26
  72.7 45.5 %all_gather.10 = f32[16,20,64]{2,1,0:T(8,128)S(1)} all-gather(f32[1,20,64]{2,1,0:T(8,128)S(1)} %exp.41), channel_id=1, replica_groups=mesh['seq'=16,'head'=2] {'seq'}, dimensions={0}, use_global_device_ids=true | all-gather | bytes 87040 | tf_op jit(solution)/shard_map/all_gather | solution.py:12
  118.2 3.2 %multiply_bitcast_fusion.1 = f32[5,256,4,64]{1,3,2,0:T(8,128)} fusion(f32[256,5,4,64]{0,3,2,1:T(8,128)} %reshape.89, f32[256,5,4,64]{0,3,2,1:T(8,128)} %bitcast.108), kind=kLoop, calls=%fused_computation.39 | loop fusion | flops 327680 | bytes 3932160 | tf_op jit(solution)/shard_map/transpose | solution.py:26
  122.6 24.7 %while.25 = (s32[]{:T(128)}, f32[5,256,4,64]{1,3,2,0:T(8,128)}, f32[5,256,4,64]{1,3,2,0:T(8,128)}, f32[5,256,4,64]{1,3,2,0:T(8,128)}, f32[5,256,4,64]{1,3,2,0:T(8,128)}, /*index=5*/s32[]{:T(128)}) while((s32[]{:T(128)}, f32[5,256,4,64]{1,3,2,0:T(8,128)}, f32[5,256,4,64]{1,3,2,0:T(8,128)}, f32[5,256,4,64]{1,3,2,0:T(8,128)}, ...), condition=%wide.region_1.2_spmd.clone, body=%wide.region_0.1_spmd.clone.sunk | while | flops 402980864 | bytes 3278917 | solution.py:65
  122.6 2.1 %convolution_select_fusion.2 = f32[4,256,256]{2,1,0:T(8,128)S(1)} fusion(pred[256,256]{1,0:T(8,128)(4,1)S(1)} %iota_compare_fusion.4, f32[5,256,4,64]{1,3,2,0:T(8,128)} %get-tuple-element.275, s32[]{:T(128)} %get-tuple-element.265, f32[5,256,4,64]{1,3,2,0:T(8,128)} %get-tuple-element.274), kind=kOutput, calls=%fused_computation.1.clone.1 | convolution fusion | flops 201588736 | bytes 1639424 | tf_op jit(solution)/shard_map/while/body/eval_jaxpr/thc,shc->hts/dot_general | solution.py:61
  124.8 2.8 %fusion.44 = f32[5,256,4,64]{1,3,2,0:T(8,128)} fusion(f32[5,256,4,64]{1,3,2,0:T(8,128)} %get-tuple-element.266, s32[]{:T(128)} %get-tuple-element.265, f32[4,256,256]{2,1,0:T(8,128)S(1)} %convolution_select_fusion.2, f32[5,256,4,64]{1,3,2,0:T(8,128)} %get-tuple-element.273), kind=kOutput, calls=%fused_computation.3.clone.1 | convolution fusion | flops 201326592 | bytes 1573888 | tf_op jit(solution)/shard_map/while/body/eval_jaxpr/hts,shj->thj/dot_general | solution.py:63
  129.7 2.8 %fusion.44 = f32[5,256,4,64]{1,3,2,0:T(8,128)} fusion(f32[5,256,4,64]{1,3,2,0:T(8,128)} %get-tuple-element.266, s32[]{:T(128)} %get-tuple-element.265, f32[4,256,256]{2,1,0:T(8,128)S(1)} %convolution_select_fusion.2, f32[5,256,4,64]{1,3,2,0:T(8,128)} %get-tuple-element.273), kind=kOutput, calls=%fused_computation.3.clone.1 | convolution fusion | flops 201326592 | bytes 1573888 | tf_op jit(solution)/shard_map/while/body/eval_jaxpr/hts,shj->thj/dot_general | solution.py:63
  132.5 2.1 %convolution_select_fusion.2 = f32[4,256,256]{2,1,0:T(8,128)S(1)} fusion(pred[256,256]{1,0:T(8,128)(4,1)S(1)} %iota_compare_fusion.4, f32[5,256,4,64]{1,3,2,0:T(8,128)} %get-tuple-element.275, s32[]{:T(128)} %get-tuple-element.265, f32[5,256,4,64]{1,3,2,0:T(8,128)} %get-tuple-element.274), kind=kOutput, calls=%fused_computation.1.clone.1 | convolution fusion | flops 201588736 | bytes 1639424 | tf_op jit(solution)/shard_map/while/body/eval_jaxpr/thc,shc->hts/dot_general | solution.py:61
  134.6 2.8 %fusion.44 = f32[5,256,4,64]{1,3,2,0:T(8,128)} fusion(f32[5,256,4,64]{1,3,2,0:T(8,128)} %get-tuple-element.266, s32[]{:T(128)} %get-tuple-element.265, f32[4,256,256]{2,1,0:T(8,128)S(1)} %convolution_select_fusion.2, f32[5,256,4,64]{1,3,2,0:T(8,128)} %get-tuple-element.273), kind=kOutput, calls=%fused_computation.3.clone.1 | convolution fusion | flops 201326592 | bytes 1573888 | tf_op jit(solution)/shard_map/while/body/eval_jaxpr/hts,shj->thj/dot_general | solution.py:63
  139.6 2.8 %fusion.44 = f32[5,256,4,64]{1,3,2,0:T(8,128)} fusion(f32[5,256,4,64]{1,3,2,0:T(8,128)} %get-tuple-element.266, s32[]{:T(128)} %get-tuple-element.265, f32[4,256,256]{2,1,0:T(8,128)S(1)} %convolution_select_fusion.2, f32[5,256,4,64]{1,3,2,0:T(8,128)} %get-tuple-element.273), kind=kOutput, calls=%fused_computation.3.clone.1 | convolution fusion | flops 201326592 | bytes 1573888 | tf_op jit(solution)/shard_map/while/body/eval_jaxpr/hts,shj->thj/dot_general | solution.py:63
  142.4 2.1 %convolution_select_fusion.2 = f32[4,256,256]{2,1,0:T(8,128)S(1)} fusion(pred[256,256]{1,0:T(8,128)(4,1)S(1)} %iota_compare_fusion.4, f32[5,256,4,64]{1,3,2,0:T(8,128)} %get-tuple-element.275, s32[]{:T(128)} %get-tuple-element.265, f32[5,256,4,64]{1,3,2,0:T(8,128)} %get-tuple-element.274), kind=kOutput, calls=%fused_computation.1.clone.1 | convolution fusion | flops 201588736 | bytes 1639424 | tf_op jit(solution)/shard_map/while/body/eval_jaxpr/thc,shc->hts/dot_general | solution.py:61
  144.5 2.8 %fusion.44 = f32[5,256,4,64]{1,3,2,0:T(8,128)} fusion(f32[5,256,4,64]{1,3,2,0:T(8,128)} %get-tuple-element.266, s32[]{:T(128)} %get-tuple-element.265, f32[4,256,256]{2,1,0:T(8,128)S(1)} %convolution_select_fusion.2, f32[5,256,4,64]{1,3,2,0:T(8,128)} %get-tuple-element.273), kind=kOutput, calls=%fused_computation.3.clone.1 | convolution fusion | flops 201326592 | bytes 1573888 | tf_op jit(solution)/shard_map/while/body/eval_jaxpr/hts,shj->thj/dot_general | solution.py:63
  147.3 2.9 %fusion.15 = f32[256,20,64]{0,2,1:T(8,128)} fusion(f32[256,20,64]{0,2,1:T(8,128)} %bitcast.15, bf16[256,20,64]{0,2,1:T(8,128)(2,1)} %copy-done.2, f32[256,20,64]{0,2,1:T(8,128)S(1)} %reshape.92, f32[256,20,64]{0,2,1:T(8,128)S(1)} %reshape.91, f32[20,64]{1,0:T(8,128)S(1)} %constant_dynamic-slice_fusion), kind=kOutput, calls=%fused_computation.20 | output fusion | flops 1643583 | bytes 5903360 | tf_op jit(solution)/shard_map/mul | solution.py:75
  150.2 23.4 %all-gather.3.cloned.1.call-done = f32[320,64,64]{2,1,0:T(8,128)} async-done(((f32[20,64,64]{2,1,0:T(8,128)}), f32[320,64,64]{2,1,0:T(8,128)}) %all-gather.3.cloned.1.call-update) | async-done | bytes 5242896 | tf_op jit(solution)/shard_map/all_gather | solution.py:12
  173.6 23.2 %while.26 = (s32[]{:T(128)}, f32[20,64,64]{2,1,0:T(8,128)S(1)}, s32[]{:T(128)}, f32[16,20,64]{2,1,0:T(8,128)S(1)}, f32[16,20,64,64]{3,2,1,0:T(8,128)}, /*index=5*/s32[]{:T(128)}, s32[]{:T(128)}) while((s32[]{:T(128)}, f32[20,64,64]{2,1,0:T(8,128)S(1)}, s32[]{:T(128)}, f32[16,20,64]{2,1,0:T(8,128)S(1)}, ...), condition=%wide.region_4.5_spmd.clone, body=%wide.region_3.4_spmd.clone.sunk | while | flops 327684 | bytes 998505 | solution.py:21
  196.9 3.2 %fusion.29 = (f32[256,20]{0,1:T(8,128)S(1)}, f32[256,20,64]{0,2,1:T(8,128)S(1)}) fusion(f32[256,20,64]{0,2,1:T(8,128)} %fusion.15, f32[20,64,64]{2,1,0:T(8,128)S(1)} %get-tuple-element.132, f32[256,20,64]{0,2,1:T(8,128)S(1)} %reshape.91, f32[256,20,64]{0,2,1:T(8,128)} %bitcast.109), kind=kOutput, calls=%fused_computation.56 | convolution fusion | flops 252636160 | bytes 5591040 | tf_op jit(solution)/shard_map/thc,hcj->thj/dot_general | solution.py:85
  200.9 2.4 %fusion.17 = bf16[256,1280]{1,0:T(8,128)(2,1)} fusion(bf16[128,2,1280]{2,0,1:T(8,128)(2,1)} %all-to-all-done.4, f32[256,1280]{1,0:T(8,128)S(1)} %copy.49, f32[1280]{0:T(1024)S(1)} %dynamic_slice.35, f32[1280]{0:T(1024)S(1)} %dynamic_slice.34), kind=kLoop, calls=%fused_computation.24 | loop fusion | flops 2949120 | bytes 2631680 | tf_op jit(solution)/shard_map/convert_element_type | solution.py:93
  (90 shorter events, 43.3 us)
Async XLA Ops:
  6.5 111.6 %copy-start = (f32[40,64]{1,0:T(8,128)S(1)}, f32[40,64]{1,0:T(8,128)}, u32[]{:S(2)}) copy-start(f32[40,64]{1,0:T(8,128)} %param.17) | copy-start | bytes 30724
  6.5 5.6 %copy-start.6 = (bf16[128,2560]{1,0:T(8,128)(2,1)S(1)}, bf16[128,2560]{1,0:T(8,128)(2,1)}, u32[]{:S(2)}) copy-start(bf16[128,2560]{1,0:T(8,128)(2,1)} %param.13) | copy-start | bytes 1966084
  8.6 5.3 %all-to-all-start.2 = ((bf16[128,2,1280]{2,0,1:T(8,128)(2,1)}), bf16[128,2,1280]{2,0,1:T(8,128)(2,1)S(1)}, u32[]{:S(2)}, u32[]{:S(2)}) async-start(bf16[128,2,1280]{2,0,1:T(8,128)(2,1)} %bitcast.93), calls=%async_computation.2 | async-start | bytes 1310720 | tf_op jit(solution)/shard_map/all_to_all | solution.py:115
  13.9 8.0 %all-to-all-start.3 = ((bf16[128,2,1280]{0,2,1:T(8,128)(2,1)}), bf16[128,2,1280]{0,2,1:T(8,128)(2,1)S(1)}, u32[]{:S(2)}, u32[]{:S(2)}) async-start(bf16[128,2,1280]{0,2,1:T(8,128)(2,1)} %bitcast.10), calls=%async_computation.3 | async-start | bytes 1310720 | tf_op jit(solution)/shard_map/all_to_all | solution.py:108
  19.5 1.5 copy-start.7
  21.9 8.4 %all-to-all-start = ((bf16[2,128,1280]{2,1,0:T(8,128)(2,1)}), bf16[2,128,1280]{2,1,0:T(8,128)(2,1)S(1)}, u32[]{:S(2)}, u32[]{:S(2)}) async-start(bf16[2,128,1280]{2,1,0:T(8,128)(2,1)} %pad_maximum_fusion), calls=%async_computation | async-start | bytes 1310720 | tf_op jit(solution)/shard_map/all_to_all | solution.py:110
  25.4 148.2 %all-gather.3.cloned.1.call-start = ((), (), s32[]{:S(2)}) async-start(), calls=%async_computation.5 | async-start | bytes 11141120 | tf_op jit(solution)/shard_map/all_gather | solution.py:12
  30.4 1.0 copy-start.3
  31.7 1.1 copy-start.2
  38.2 7.6 %all-to-all-start.1 = ((bf16[128,2,1280]{0,2,1:T(8,128)(2,1)}), bf16[128,2,1280]{0,2,1:T(8,128)(2,1)S(1)}, u32[]{:S(2)}, u32[]{:S(2)}) async-start(bf16[128,2,1280]{0,2,1:T(8,128)(2,1)} %bitcast.3), calls=%async_computation.1 | async-start | bytes 1310720 | tf_op jit(solution)/shard_map/all_to_all | solution.py:107
  45.8 155.1 %all-to-all-start.4 = ((bf16[128,2,1280]{2,0,1:T(8,128)(2,1)}), bf16[128,2,1280]{2,0,1:T(8,128)(2,1)}, u32[]{:S(2)}, u32[]{:S(2)}) async-start(bf16[128,2,1280]{2,0,1:T(8,128)(2,1)} %bitcast.92), calls=%async_computation.4 | async-start | bytes 1310720 | tf_op jit(solution)/shard_map/all_to_all | solution.py:116
  55.1 1.1 copy-start.1
  69.3 3.2 %copy-start.8 = (f32[2560]{0:T(1024)S(1)}, f32[2560]{0:T(1024)}, u32[]{:S(2)}) copy-start(f32[2560]{0:T(1024)} %param.18) | copy-start | bytes 30724
  69.3 3.3 %copy-start.9 = (f32[2560]{0:T(1024)S(1)}, f32[2560]{0:T(1024)}, u32[]{:S(2)}) copy-start(f32[2560]{0:T(1024)} %param.19) | copy-start | bytes 30724
  118.2 3.2 %copy-start.4 = (f32[256,5,4,64]{0,3,2,1:T(8,128)S(1)}, f32[256,5,4,64]{0,3,2,1:T(8,128)}, u32[]{:S(2)}) copy-start(f32[256,5,4,64]{0,3,2,1:T(8,128)} %reshape.90) | copy-start | bytes 3932164
  118.2 3.2 %copy-start.5 = (f32[256,1280]{0,1:T(8,128)S(1)}, f32[256,1280]{0,1:T(8,128)}, u32[]{:S(2)}) copy-start(f32[256,1280]{0,1:T(8,128)} %copy.42) | copy-start | bytes 3932164
Sparse Core Ops, SparseCore 0:
  36.1 137.4 all-gather.2
